TPU v7x, 32 devices: a whole 2x2x4 slice. The times are simulated.
32 devices in a mesh: section: 4 (over z), dp: 4 (over y, x), mp: 2 (over core).
Axes of the slice: x: 2, y: 2, z: 4, core: 2. Of those that a mesh axis runs over, the one named last changes fastest.
Arguments:
- fwd_in: bfloat16 [4, 2048, 1024], P('section', ('dp', 'mp')), may hold values from -6 to 6
- stash: bfloat16 [4, 2048, 1024], P('section', ('dp', 'mp')), may hold values from -6 to 6
- cot: bfloat16 [4, 2048, 1024], P('section', ('dp', 'mp')), may hold values from -8 to 8
- w_in: bfloat16 [4, 2048, 1024], P('section', 'mp'), may hold values from -0.1875 to 0.1875
- w_out: bfloat16 [4, 2048, 1024], P('section', 'mp'), may hold values from -0.125 to 0.125
- gain: float32 [4, 1024], P('section'), may hold values from 0.1 to 1.9
Outputs:
- passed_fwd: bfloat16 [4, 2048, 1024], P('section', ('dp', 'mp'))
- passed_grad: bfloat16 [4, 2048, 1024], P('section', ('dp', 'mp'))
- grad_w_in: bfloat16 [4, 2048, 1024], P('section', 'mp', 'dp')
- grad_w_out: bfloat16 [4, 2048, 1024], P('section', 'mp', 'dp')
All inputs are finite; a program needn't handle non-finite values.
Results may differ from a plain program's by a relative error of at most 0.015.
Values may be sent and summed in bfloat16 or wider, within the bound.
A program may use at most 64 MiB of HBM per device.

v0:
```python
import jax
import jax.numpy as jnp
from jax import lax
from jax.sharding import PartitionSpec as P

norm_eps = 1e-05
gelu_coef = 0.7978845608


def shifted(x, axis, by):
    length = lax.axis_size(axis)
    return lax.ppermute(x, axis, [(i, (i + by) % length) for i in range(length)])


def gelu_value(v):
    inner = jnp.tanh(gelu_coef * (v + 0.044715 * v * v * v))
    return 0.5 * v * (1.0 + inner)


def gelu_slope(v):
    inner = jnp.tanh(gelu_coef * (v + 0.044715 * v * v * v))
    return 0.5 * (1.0 + inner) + 0.5 * v * (1.0 - inner * inner) * gelu_coef * (
        1.0 + 0.134145 * v * v
    )


def prepare(x, w_first, gain_row):
    xf = x.astype(jnp.float32)
    scale = lax.rsqrt(jnp.mean(xf * xf, axis=-1, keepdims=True) + norm_eps)
    normed = (xf * scale * gain_row[None, :]).astype(jnp.bfloat16)
    pre = lax.dot_general(
        normed, w_first, (((1,), (1,)), ((), ())), preferred_element_type=jnp.float32
    )
    act = gelu_value(pre).astype(jnp.bfloat16)
    return (scale, normed, pre, act)


def on_device(fwd_in, stash, cot, w_in, w_out, gain):
    x_fwd = fwd_in[0]
    x_bwd = stash[0]
    cot_local = cot[0]
    w_first = w_in[0]
    w_second = w_out[0]
    gain_row = gain[0]
    local_rows = x_fwd.shape[0]
    scale, normed, pre, act = prepare(
        lax.all_gather(x_fwd, "mp", axis=0, tiled=True), w_first, gain_row
    )
    terms = jnp.dot(act, w_second, preferred_element_type=jnp.float32)
    branch = lax.psum_scatter(
        terms.astype(jnp.bfloat16), "mp", scatter_dimension=0, tiled=True
    ).astype(jnp.float32)
    out = (x_fwd.astype(jnp.float32) + branch).astype(jnp.bfloat16)
    passed_fwd = shifted(out, "section", 1)
    rows_x, rows_cot = (
        lax.all_gather(x_bwd, "mp", axis=0, tiled=True),
        lax.all_gather(cot_local, "mp", axis=0, tiled=True),
    )
    scale, normed, pre, act = prepare(rows_x, w_first, gain_row)
    d_act = lax.dot_general(
        rows_cot, w_second, (((1,), (1,)), ((), ())), preferred_element_type=jnp.float32
    )
    d_pre = (d_act * gelu_slope(pre)).astype(jnp.bfloat16)
    d_norm = lax.psum_scatter(
        jnp.dot(d_pre, w_first, preferred_element_type=jnp.float32).astype(jnp.bfloat16),
        "mp",
        scatter_dimension=0,
        tiled=True,
    ).astype(jnp.float32)
    offset = lax.axis_index("mp") * local_rows
    own_scale = lax.dynamic_slice_in_dim(scale, offset, local_rows, 0)
    shard_x = x_bwd.astype(jnp.float32)
    push = d_norm * gain_row[None, :]
    mixed = jnp.mean(shard_x * push, axis=-1, keepdims=True)
    dx = (
        cot_local.astype(jnp.float32)
        + own_scale * push
        - shard_x * own_scale * own_scale * own_scale * mixed
    )
    passed_grad = shifted(dx.astype(jnp.bfloat16), "section", -1)
    term_out = lax.dot_general(
        act, rows_cot, (((0,), (0,)), ((), ())), preferred_element_type=jnp.float32
    )
    term_in = lax.dot_general(
        d_pre, normed, (((0,), (0,)), ((), ())), preferred_element_type=jnp.float32
    )
    sum_in, sum_out = (
        lax.psum_scatter(
            term_in.astype(jnp.bfloat16), "dp", scatter_dimension=1, tiled=True
        ).astype(jnp.float32),
        lax.psum_scatter(
            term_out.astype(jnp.bfloat16), "dp", scatter_dimension=1, tiled=True
        ).astype(jnp.float32),
    )
    return (
        passed_fwd[None],
        passed_grad[None],
        sum_in.astype(jnp.bfloat16)[None],
        sum_out.astype(jnp.bfloat16)[None],
    )


def solution(mesh):
    in_specs = (
        P("section", ("dp", "mp"), None),
        P("section", ("dp", "mp"), None),
        P("section", ("dp", "mp"), None),
        P("section", "mp", None),
        P("section", "mp", None),
        P("section", None),
    )
    out_specs = (
        P("section", ("dp", "mp"), None),
        P("section", ("dp", "mp"), None),
        P("section", "mp", "dp"),
        P("section", "mp", "dp"),
    )
    return jax.shard_map(
        on_device, mesh=mesh, in_specs=in_specs, out_specs=out_specs, check_vma=False
    )
```

profile of v0, /device:TPU:0, one launch (start us, length us, event | category | flops | bytes accessed | tf_op | source)
XLA Modules:
  0.0 155.3 jit_solution(14165824930443824709)
XLA Ops:
  9.5 11.9 %all-gather.9.cloned.1.call-done = bf16[1,512,1024]{2,1,0:T(8,128)(2,1)} async-done(((bf16[1,256,1024]{2,1,0:T(8,128)(2,1)}), bf16[1,512,1024]{2,1,0:T(8,128)(2,1)}) %all-gather.9.cloned.1.call-update) | async-done | bytes 1048592 | tf_op jit(solution)/shard_map/all_gather | solution.py:56
  21.3 1.5 fusion.3
  22.9 3.9 %fusion.24 = f32[512,1024]{1,0:T(8,128)} fusion(bf16[1,1024,1024]{2,1,0:T(8,128)(2,1)S(1)} %copy-done, bf16[1,512,1024]{2,1,0:T(8,128)(2,1)} %all-gather.9.cloned.1.call-done, f32[512]{0:T(512)S(1)} %add_rsqrt_fusion, f32[1024]{0:T(1024)S(1)} %bitcast.61), kind=kOutput, calls=%fused_computation.31 | convolution fusion | flops 1075838976 | bytes 5249024 | tf_op jit(solution)/shard_map/dot_general | solution.py:31
  26.7 6.4 %all-gather.11.cloned.1.call-done = bf16[1,512,1024]{2,1,0:T(8,128)(2,1)} async-done(((bf16[1,256,1024]{2,1,0:T(8,128)(2,1)}), bf16[1,512,1024]{2,1,0:T(8,128)(2,1)}) %all-gather.11.cloned.1.call-update) | async-done | bytes 1048592 | tf_op jit(solution)/shard_map/all_gather | solution.py:57
  33.1 4.7 %fusion.17 = bf16[512,1024]{1,0:T(8,128)(2,1)S(1)} fusion(f32[512,1024]{1,0:T(8,128)} %fusion.24, bf16[1,1024,1024]{2,1,0:T(8,128)(2,1)} %param.10, bf16[1,512,1024]{2,1,0:T(8,128)(2,1)} %all-gather.11.cloned.1.call-done), kind=kOutput, calls=%fused_computation.24 | convolution fusion | flops 1083703296 | bytes 6291456 | tf_op jit(solution)/shard_map/dot_general | solution.py:60
  37.9 1.0 copy-done.6
  38.9 2.3 %fusion.28 = bf16[512,1024]{1,0:T(8,128)(2,1)} fusion(bf16[512,1024]{1,0:T(8,128)(2,1)S(1)} %fusion.17, bf16[1,1024,1024]{2,1,0:T(8,128)(2,1)S(1)} %copy-done), kind=kOutput, calls=%fused_computation.38 | convolution fusion | flops 1074266112 | bytes 4194304 | tf_op jit(solution)/shard_map/dot_general | solution.py:65
  41.3 3.6 %all-gather.7.cloned.1.call-done = bf16[1,512,1024]{2,1,0:T(8,128)(2,1)} async-done(((bf16[1,256,1024]{2,1,0:T(8,128)(2,1)}), bf16[1,512,1024]{2,1,0:T(8,128)(2,1)}) %all-gather.7.cloned.1.call-update) | async-done | bytes 1048592 | tf_op jit(solution)/shard_map/all_gather | solution.py:47
  44.9 1.5 fusion
  46.4 5.4 %fusion.31 = bf16[512,1024]{1,0:T(8,128)(2,1)} fusion(bf16[1,1024,1024]{2,1,0:T(8,128)(2,1)} %param.10, bf16[1,1024,1024]{2,1,0:T(8,128)(2,1)S(1)} %copy-done, bf16[1,512,1024]{2,1,0:T(8,128)(2,1)} %all-gather.7.cloned.1.call-done, f32[1024]{0:T(1024)S(1)} %bitcast.62, f32[512]{0:T(512)S(1)} %add_rsqrt_fusion.1), kind=kOutput, calls=%fused_computation.39 | convolution fusion | flops 2154823680 | bytes 6297600 | tf_op jit(solution)/shard_map/dot_general | solution.py:49
  51.9 3.9 %convolution_convert_fusion.1 = bf16[1024,1024]{1,0:T(8,128)(2,1)} fusion(bf16[512,1024]{1,0:T(8,128)(2,1)} %copy-done.6, bf16[1,512,1024]{2,1,0:T(8,128)(2,1)S(1)} %copy-done.3, f32[512]{0:T(512)S(1)} %add_rsqrt_fusion, f32[1024]{0:T(1024)S(1)} %bitcast.63), kind=kOutput, calls=%fused_computation.37 | convolution fusion | flops 1076887552 | bytes 4200448 | tf_op jit(solution)/shard_map/dot_general | solution.py:84
  55.9 1.2 copy-done.5
  57.1 4.4 %convolution_convert_fusion = bf16[1024,1024]{1,0:T(8,128)(2,1)} fusion(f32[512,1024]{1,0:T(8,128)} %fusion.24, bf16[1,512,1024]{2,1,0:T(8,128)(2,1)S(1)} %copy-done.5), kind=kOutput, calls=%fused_computation.36 | convolution fusion | flops 1079508992 | bytes 5242880 | tf_op jit(solution)/shard_map/dot_general | solution.py:81
  61.6 0.9 copy-done.1
  62.5 1.3 fusion.43
  63.9 2.3 %fusion.42 = bf16[256,1024]{1,0:T(8,128)(2,1)} fusion(bf16[256,1024]{1,0:T(8,128)(2,1)} %reduce-scatter.7.cloned.1.call-done, bf16[1,256,1024]{2,1,0:T(8,128)(2,1)S(1)} %copy-done.2, bf16[1,256,1024]{2,1,0:T(8,128)(2,1)S(1)} %copy-done.1, f32[256]{0:T(256)S(1)} %broadcast_multiply_fusion, f32[1024]{0:T(1024)S(1)} %bitcast.65, f32[256]{0:T(256)S(1)} %dynamic-slice.3), kind=kLoop, calls=%fused_computation.46 | loop fusion | flops 3145728 | bytes 2103296 | tf_op jit(solution)/shard_map/convert_element_type | solution.py:80
  66.1 3.6 %collective-permute-start.1 = (bf16[256,1024]{1,0:T(8,128)(2,1)}, bf16[256,1024]{1,0:T(8,128)(2,1)S(1)}, u32[]{:S(2)}, u32[]{:S(2)}) collective-permute-start(bf16[256,1024]{1,0:T(8,128)(2,1)} %fusion.42), channel_id=1, source_target_pairs={{0,24},{8,0},{16,8},{24,16},{1,25},{9,1},{17,9},{25,17},{2,26},{10... | collective-permute-start | bytes 1572872 | tf_op jit(solution)/shard_map/ppermute | solution.py:12
  69.7 1.4 fusion.45
  71.5 10.8 %collective-permute-done.1 = bf16[256,1024]{1,0:T(8,128)(2,1)S(1)} collective-permute-done((bf16[256,1024]{1,0:T(8,128)(2,1)}, bf16[256,1024]{1,0:T(8,128)(2,1)S(1)}, u32[]{:S(2)}, u32[]{:S(2)}) %collective-permute-start.1) | collective-permute-done | bytes 524320 | tf_op jit(solution)/shard_map/ppermute | solution.py:12
  82.4 11.4 %collective-permute-done = bf16[256,1024]{1,0:T(8,128)(2,1)S(1)} collective-permute-done((bf16[256,1024]{1,0:T(8,128)(2,1)S(1)}, bf16[256,1024]{1,0:T(8,128)(2,1)S(1)}, u32[]{:S(2)}, u32[]{:S(2)}) %collective-permute-start) | collective-permute-done | bytes 524320 | tf_op jit(solution)/shard_map/ppermute | solution.py:12
  93.8 14.3 %reduce-scatter.9.cloned.1.call-done = bf16[1024,256]{1,0:T(8,128)(2,1)} async-done(((bf16[1024,1024]{1,0:T(8,128)(2,1)}), bf16[1024,256]{1,0:T(8,128)(2,1)}) %reduce-scatter.9.cloned.1.call-update) | async-done | bytes 524304 | tf_op jit(solution)/shard_map/reduce_scatter | solution.py:88
  108.1 38.7 %reduce-scatter.11.cloned.1.call-done = bf16[1024,256]{1,0:T(8,128)(2,1)} async-done(((bf16[1024,1024]{1,0:T(8,128)(2,1)}), bf16[1024,256]{1,0:T(8,128)(2,1)}) %reduce-scatter.11.cloned.1.call-update) | async-done | bytes 524304 | tf_op jit(solution)/shard_map/reduce_scatter | solution.py:91
  146.9 0.8 copy.12
  147.7 0.8 copy.13
  (32 shorter events, 3.0 us)
Async XLA Ops:
  7.2 15.7 %copy-start = (bf16[1,1024,1024]{2,1,0:T(8,128)(2,1)S(1)}, bf16[1,1024,1024]{2,1,0:T(8,128)(2,1)}, u32[]{:S(2)}) copy-start(bf16[1,1024,1024]{2,1,0:T(8,128)(2,1)} %param.9) | copy-start | bytes 6291460
  7.2 15.7 %copy-start.4 = (f32[1,1024]{1,0:T(1,128)S(1)}, f32[1,1024]{1,0:T(1,128)}, u32[]{:S(2)}) copy-start(f32[1,1024]{1,0:T(1,128)} %param.11) | copy-start | bytes 12292
  7.2 14.1 %all-gather.9.cloned.1.call-start = ((), (), s32[]{:S(2)}) async-start(), calls=%async_computation.9 | async-start | bytes 1572864 | tf_op jit(solution)/shard_map/all_gather | solution.py:56
  7.9 25.2 %all-gather.11.cloned.1.call-start = ((), (), s32[]{:S(2)}) async-start(), calls=%async_computation.10 | async-start | bytes 1572864 | tf_op jit(solution)/shard_map/all_gather | solution.py:57
  8.7 36.2 %all-gather.7.cloned.1.call-start = ((), (), s32[]{:S(2)}) async-start(), calls=%async_computation.8 | async-start | bytes 1572864 | tf_op jit(solution)/shard_map/all_gather | solution.py:47
  9.4 52.2 %reduce-scatter.7.cloned.1.call-start = ((), (), s32[]{:S(2)}) async-start(), calls=%async_computation.5 | async-start | bytes 1572864 | tf_op jit(solution)/shard_map/reduce_scatter | solution.py:64
  37.9 1.1 copy-start.6
  41.2 28.5 %reduce-scatter.5.cloned.1.call-start = ((), (), s32[]{:S(2)}) async-start(), calls=%async_computation.4 | async-start | bytes 1572864 | tf_op jit(solution)/shard_map/reduce_scatter | solution.py:50
  46.4 5.5 %copy-start.3 = (bf16[1,512,1024]{2,1,0:T(8,128)(2,1)S(1)}, bf16[1,512,1024]{2,1,0:T(8,128)(2,1)}, u32[]{:S(2)}) copy-start(bf16[1,512,1024]{2,1,0:T(8,128)(2,1)} %all-gather.9.cloned.1.call-done) | copy-start | bytes 3145732
  51.9 56.3 %reduce-scatter.9.cloned.1.call-start = ((), (), s32[]{:S(2)}) async-start(), calls=%async_computation.6 | async-start | bytes 2621440 | tf_op jit(solution)/shard_map/reduce_scatter | solution.py:88
  55.8 1.3 copy-start.5
  55.9 91.0 %reduce-scatter.11.cloned.1.call-start = ((), (), s32[]{:S(2)}) async-start(), calls=%async_computation.7 | async-start | bytes 2621440 | tf_op jit(solution)/shard_map/reduce_scatter | solution.py:91
  61.5 1.0 copy-start.1
  61.5 2.3 %copy-start.2 = (bf16[1,256,1024]{2,1,0:T(8,128)(2,1)S(1)}, bf16[1,256,1024]{2,1,0:T(8,128)(2,1)}, u32[]{:S(2)}) copy-start(bf16[1,256,1024]{2,1,0:T(8,128)(2,1)} %param.8) | copy-start | bytes 1572868
  66.1 16.3 %collective-permute-start.1 = (bf16[256,1024]{1,0:T(8,128)(2,1)}, bf16[256,1024]{1,0:T(8,128)(2,1)S(1)}, u32[]{:S(2)}, u32[]{:S(2)}) collective-permute-start(bf16[256,1024]{1,0:T(8,128)(2,1)} %fusion.42), channel_id=1, source_target_pairs={{0,24},{8,0},{16,8},{24,16},{1,25},{9,1},{17,9},{25,17},{2,26},{10... | collective-permute-start | bytes 1572872 | tf_op jit(solution)/shard_map/ppermute | solution.py:12
  71.1 22.7 %collective-permute-start = (bf16[256,1024]{1,0:T(8,128)(2,1)S(1)}, bf16[256,1024]{1,0:T(8,128)(2,1)S(1)}, u32[]{:S(2)}, u32[]{:S(2)}) collective-permute-start(bf16[256,1024]{1,0:T(8,128)(2,1)S(1)} %fusion.45), channel_id=1, source_target_pairs={{0,8},{8,16},{16,24},{24,0},{1,9},{9,17},{17,25},{25,1},{2,10},{10... | collective-permute-start | bytes 1572872 | tf_op jit(solution)/shard_map/ppermute | solution.py:12
Sparse Core Ops, SparseCore 0:
  9.5 11.7 all-gather.8
  22.9 10.1 all-gather.10
  34.7 10.1 all-gather.6
  47.0 9.5 reduce-scatter.6
  58.6 9.5 reduce-scatter.4
  71.7 36.4 reduce-scatter.8
  111.7 35.1 reduce-scatter.10
where the time goes:
time: 156 us; the launch traced here: 155 us
  waiting for transfers between devices  99.3 us (64%)
  matrix products  24.6 us (16%)
  between operations  14.2 us (9%)
  other arithmetic  7.98 us (5%)
  local copies, waits for them, and re-layouts  4.85 us (3%)
  starting transfers between devices  4.29 us (3%)
    reduce_scatter x1, waiting for transfers between devices, on_device(): lax.psum_scatter(term_out.astype(jnp.bfloat16), 'dp', scatter_dimension=1...  38.7 us
    ppermute x2, waiting for transfers between devices, shifted(): lax.ppermute(x, axis, [(i, (i + by) % length) for i in range(length)])  22.3 us
    reduce_scatter x1, waiting for transfers between devices, on_device(): lax.psum_scatter(term_in.astype(jnp.bfloat16), 'dp', scatter_dimension=1,...  14.3 us
    all_gather x1, waiting for transfers between devices, on_device(): lax.all_gather(x_bwd, 'mp', axis=0, tiled=True)  11.9 us
    all_gather x1, waiting for transfers between devices, on_device(): lax.all_gather(cot_local, 'mp', axis=0, tiled=True)  6.37 us
    dot_general x1, matrix products, on_device(): terms = jnp.dot(act, w_second, preferred_element_type=jnp.float32)  5.42 us
    unnamed x16, local copies, waits for them, and re-layouts  4.77 us
    dot_general x1, matrix products, on_device(): lax.dot_general(rows_cot, w_second, (((1,), (1,)), ((), ())), preferred_e...  4.75 us
  transfers between devices with their start and end apart: 9, of which 7 were waited for; matrix products, arithmetic and copies ran while one was open for 21% of the time, Pallas kernels for 0%

commit v1 on v0

--- a/solution.py
+++ b/solution.py
@@ -1,6 +1,8 @@
 import jax
 import jax.numpy as jnp
 from jax import lax
+from jax.experimental import pallas as pl
+from jax.experimental.pallas import tpu as pltpu
 from jax.sharding import PartitionSpec as P
 
 norm_eps = 1e-05
@@ -100,6 +102,301 @@
     )
 
 
+MESH = pl.DeviceIdType.MESH
+NT = (((1,), (1,)), ((), ()))
+TN = (((0,), (0,)), ((), ()))
+DIAG, DIRECT, SECOND, OWN = range(4)
+OUT, IN = range(2)
+
+
+def tile_of(total, most):
+    size = min(total, most)
+    while total % size:
+        size //= 2
+    return size
+
+
+def relay_kernel(
+    fwd_hbm, stash_hbm, cot_hbm, win_hbm, wout_hbm, gain_ref,
+    pass_fwd, pass_grad, gin_ref, gout_ref,
+    xs, xc, xf, nb, nf, win, wout, slope, act_t, dpre_t, act, parts, landed,
+    mp_out, mp_in, own_terms, z_out,
+    load_sem, mp_send, mp_recv, rs_send, rs_recv, z_send, z_recv,
+):
+    rows = stash_hbm.shape[0]
+    hid, width = win_hbm.shape
+    half = hid // 2
+    cols = gin_ref.shape[1]
+    n_sec = lax.axis_size("section")
+    sec, dp, mp = lax.axis_index("section"), lax.axis_index("dp"), lax.axis_index("mp")
+    y, x = lax.div(dp, 2), lax.rem(dp, 2)
+    flip_x, flip_y = y * 2 + (1 - x), (1 - y) * 2 + x
+    across = (1 - y) * 2 + (1 - x)
+    peer = {"mp": 1 - mp}
+    after, before = {"section": lax.rem(sec + 1, n_sec)}, {"section": lax.rem(sec + n_sec - 1, n_sec)}
+
+    own, other = pl.ds(0, rows), pl.ds(rows, rows)
+    loads = [
+        pltpu.make_async_copy(stash_hbm, xs.at[own], load_sem.at[0]),
+        pltpu.make_async_copy(win_hbm, win, load_sem.at[1]),
+        pltpu.make_async_copy(cot_hbm, xc.at[own], load_sem.at[2]),
+        pltpu.make_async_copy(wout_hbm, wout, load_sem.at[3]),
+        pltpu.make_async_copy(fwd_hbm, xf.at[own], load_sem.at[4]),
+    ]
+    for load in loads:
+        load.start()
+
+    barrier = pltpu.get_barrier_semaphore()
+    for target in (peer, {"dp": flip_x}, {"dp": flip_y}, after, before):
+        pl.semaphore_signal(barrier, inc=1, device_id=target, device_id_type=MESH)
+    pl.semaphore_wait(barrier, 5)
+
+    def remote(src, dst, send, recv, target):
+        copy = pltpu.make_async_remote_copy(
+            src_ref=src, dst_ref=dst, send_sem=send, recv_sem=recv,
+            device_id=target, device_id_type=MESH,
+        )
+        copy.start()
+        return copy
+
+    swaps = [
+        remote(src, dst.at[other], mp_send.at[i], mp_recv.at[i], peer)
+        for i, (src, dst) in enumerate(((stash_hbm, xs), (cot_hbm, xc), (fwd_hbm, xf)))
+    ]
+
+    gain = gain_ref[...]
+    step = tile_of(rows, 64)
+
+    def normalise(source, target, first):
+        def body(i, carry):
+            at = pl.ds(pl.multiple_of(first + i * step, step), step)
+            v = source[at, :].astype(jnp.float32)
+            r = lax.rsqrt(jnp.mean(v * v, axis=-1, keepdims=True) + norm_eps)
+            target[at, :] = (v * r * gain).astype(jnp.bfloat16)
+            return carry
+
+        lax.fori_loop(0, rows // step, body, 0)
+
+    block = tile_of(half, 256)
+
+    def backward_pre(slot, first, count):
+        def body(i, carry):
+            at = pl.ds(pl.multiple_of(first + i * block, block), block)
+            v = lax.dot_general(
+                win[at, :], nb[slot, :], NT, preferred_element_type=jnp.float32
+            )
+            square = v * v
+            t = jnp.tanh(gelu_coef * (v + 0.044715 * square * v))
+            act_t[at, slot] = (0.5 * v * (1.0 + t)).astype(jnp.bfloat16)
+            slope[at, slot] = 0.5 * (1.0 + t) + 0.5 * v * (1.0 - t * t) * gelu_coef * (
+                1.0 + 0.134145 * square
+            )
+            return carry
+
+        lax.fori_loop(0, count // block, body, 0)
+
+    def backward_slope(first, count):
+        def body(i, carry):
+            at = pl.ds(pl.multiple_of(first + i * block, block), block)
+            d_act = lax.dot_general(
+                wout[at, :], xc[...], NT, preferred_element_type=jnp.float32
+            )
+            dpre_t[at, :] = (d_act * slope[at, :]).astype(jnp.bfloat16)
+            return carry
+
+        lax.fori_loop(0, count // block, body, 0)
+
+    owners = (
+        (across, flip_x, flip_y, dp),
+        (across, flip_y, flip_x, dp),
+    )
+    nearest = (({"dp": flip_x}, {"dp": flip_y}), ({"dp": flip_y}, {"dp": flip_x}))
+    halves = [pl.ds(0, half), pl.ds(half, half)]
+    operands = {OUT: (act_t, xc), IN: (dpre_t, nb)}
+
+    def product(g, h, kind):
+        left, right = operands[g]
+        at = pl.ds(pl.multiple_of(owners[h][kind] * cols, cols), cols)
+        parts[g, h, kind] = jnp.dot(
+            left[halves[h], :], right[:, at], preferred_element_type=jnp.float32
+        ).astype(jnp.bfloat16)
+
+    sent = {}
+
+    def send(g, h, kind):
+        sent[g, h, kind] = remote(
+            parts.at[g, h, kind], landed.at[g, h, kind],
+            rs_send.at[g, h, kind], rs_recv.at[g, h, kind],
+            nearest[h][1 if kind == SECOND else 0],
+        )
+
+    loads[0].wait()
+    normalise(xs, nb, 0)
+    loads[1].wait()
+    backward_pre(own, 0, hid)
+    swaps[0].wait_recv()
+    normalise(xs, nb, rows)
+    backward_pre(other, 0, half)
+    loads[2].wait()
+    swaps[1].wait_recv()
+    product(OUT, 0, DIAG)
+    send(OUT, 0, DIAG)
+    backward_pre(other, half, half)
+    product(OUT, 1, DIAG)
+    send(OUT, 1, DIAG)
+    for h in range(2):
+        product(OUT, h, DIRECT)
+        send(OUT, h, DIRECT)
+
+    loads[3].wait()
+    for h in range(2):
+        backward_slope(h * half, half)
+        product(IN, h, DIAG)
+        send(IN, h, DIAG)
+    for h in range(2):
+        product(IN, h, DIRECT)
+        send(IN, h, DIRECT)
+
+    def d_norm(slot):
+        return lax.dot_general(
+            dpre_t[:, slot], win[...], TN, preferred_element_type=jnp.float32
+        ).astype(jnp.bfloat16)
+
+    mp_out[0] = d_norm(other)
+    swap_grad = remote(mp_out.at[0], mp_in.at[0], mp_send.at[3], mp_recv.at[3], peer)
+    own_terms[0] = d_norm(own)
+
+    loads[4].wait()
+
+    def forward(slot):
+        def body(i, carry):
+            at = pl.ds(pl.multiple_of(i * block, block), block)
+            v = lax.dot_general(
+                nf[slot, :], win[at, :], NT, preferred_element_type=jnp.float32
+            )
+            t = jnp.tanh(gelu_coef * (v + 0.044715 * v * v * v))
+            act[:, at] = (0.5 * v * (1.0 + t)).astype(jnp.bfloat16)
+            return carry
+
+        lax.fori_loop(0, hid // block, body, 0)
+        return jnp.dot(
+            act[...], wout[...], preferred_element_type=jnp.float32
+        ).astype(jnp.bfloat16)
+
+    swap_grad.wait_recv()
+
+    def finish_grad(i, carry):
+        at = pl.ds(pl.multiple_of(i * step, step), step)
+        v = xs[at, :].astype(jnp.float32)
+        r = lax.rsqrt(jnp.mean(v * v, axis=-1, keepdims=True) + norm_eps)
+        push = (own_terms[0, at, :].astype(jnp.float32) + mp_in[0, at, :].astype(jnp.float32)) * gain
+        mixed = jnp.mean(v * push, axis=-1, keepdims=True)
+        dx = xc[at, :].astype(jnp.float32) + r * push - v * (r * r * r * mixed)
+        z_out[0, at, :] = dx.astype(jnp.bfloat16)
+        return carry
+
+    lax.fori_loop(0, rows // step, finish_grad, 0)
+    relay_grad = remote(z_out.at[0], pass_grad, z_send.at[0], z_recv.at[0], before)
+
+    swaps[2].wait_recv()
+    normalise(xf, nf, rows)
+    mp_out[1] = forward(other)
+    swap_branch = remote(mp_out.at[1], mp_in.at[1], mp_send.at[4], mp_recv.at[4], peer)
+    normalise(xf, nf, 0)
+    own_terms[1] = forward(own)
+    swap_branch.wait_recv()
+
+    def finish_forward(i, carry):
+        at = pl.ds(pl.multiple_of(i * step, step), step)
+        branch = own_terms[1, at, :].astype(jnp.float32) + mp_in[1, at, :].astype(jnp.float32)
+        z_out[1, at, :] = (xf[at, :].astype(jnp.float32) + branch).astype(jnp.bfloat16)
+        return carry
+
+    lax.fori_loop(0, rows // step, finish_forward, 0)
+    relay_fwd = remote(z_out.at[1], pass_fwd, z_send.at[1], z_recv.at[1], after)
+
+    for g in (OUT, IN):
+        for h in range(2):
+            product(g, h, SECOND)
+        for h in range(2):
+            sent[g, h, DIAG].wait_recv()
+            parts[g, h, SECOND] = (
+                parts[g, h, SECOND].astype(jnp.float32) + landed[g, h, DIAG].astype(jnp.float32)
+            ).astype(jnp.bfloat16)
+            send(g, h, SECOND)
+        for h in range(2):
+            product(g, h, OWN)
+    for g, result in ((OUT, gout_ref), (IN, gin_ref)):
+        for h in range(2):
+            sent[g, h, DIRECT].wait_recv()
+            sent[g, h, SECOND].wait_recv()
+            result[halves[h], :] = (
+                parts[g, h, OWN].astype(jnp.float32)
+                + landed[g, h, DIRECT].astype(jnp.float32)
+                + landed[g, h, SECOND].astype(jnp.float32)
+            ).astype(jnp.bfloat16)
+
+    relay_grad.wait_recv()
+    relay_fwd.wait_recv()
+    for copy in [*swaps, swap_grad, swap_branch, relay_grad, relay_fwd, *sent.values()]:
+        copy.wait_send()
+
+
+def relay_on_device(fwd_in, stash, cot, w_in, w_out, gain):
+    rows, width = stash.shape[1:]
+    hid = w_in.shape[1]
+    tokens = rows * lax.axis_size("mp")
+    cols = width // lax.axis_size("dp")
+    half = hid // 2
+    bf16 = jnp.bfloat16
+    vmem = pl.BlockSpec(memory_space=pltpu.VMEM)
+    hbm = pl.BlockSpec(memory_space=pl.ANY)
+    shape = jax.ShapeDtypeStruct
+    results = pl.pallas_call(
+        relay_kernel,
+        out_shape=(
+            shape((rows, width), bf16), shape((rows, width), bf16),
+            shape((hid, cols), bf16), shape((hid, cols), bf16),
+        ),
+        in_specs=[hbm] * 5 + [vmem],
+        out_specs=(vmem,) * 4,
+        scratch_shapes=[
+            pltpu.VMEM((tokens, width), bf16),
+            pltpu.VMEM((tokens, width), bf16),
+            pltpu.VMEM((tokens, width), bf16),
+            pltpu.VMEM((tokens, width), bf16),
+            pltpu.VMEM((tokens, width), bf16),
+            pltpu.VMEM((hid, width), bf16),
+            pltpu.VMEM((hid, width), bf16),
+            pltpu.VMEM((hid, tokens), jnp.float32),
+            pltpu.VMEM((hid, tokens), bf16),
+            pltpu.VMEM((hid, tokens), bf16),
+            pltpu.VMEM((rows, hid), bf16),
+            pltpu.VMEM((2, 2, 4, half, cols), bf16),
+            pltpu.VMEM((2, 2, 3, half, cols), bf16),
+            pltpu.VMEM((2, rows, width), bf16),
+            pltpu.VMEM((2, rows, width), bf16),
+            pltpu.VMEM((2, rows, width), bf16),
+            pltpu.VMEM((2, rows, width), bf16),
+            pltpu.SemaphoreType.DMA((5,)),
+            pltpu.SemaphoreType.DMA((5,)),
+            pltpu.SemaphoreType.DMA((5,)),
+            pltpu.SemaphoreType.DMA((2, 2, 3)),
+            pltpu.SemaphoreType.DMA((2, 2, 3)),
+            pltpu.SemaphoreType.DMA((2,)),
+            pltpu.SemaphoreType.DMA((2,)),
+        ],
+        compiler_params=pltpu.CompilerParams(
+            collective_id=0, has_side_effects=True, vmem_limit_bytes=56 * 2**20
+        ),
+    )(fwd_in[0], stash[0], cot[0], w_in[0], w_out[0], gain)
+    return tuple(r[None] for r in results)
+
+
+def fits_relay(mesh):
+    return mesh.shape["dp"] == 4 and mesh.shape["mp"] == 2 and mesh.shape["section"] > 1
+
+
 def solution(mesh):
     in_specs = (
         P("section", ("dp", "mp"), None),
@@ -116,5 +413,9 @@
         P("section", "mp", "dp"),
     )
     return jax.shard_map(
-        on_device, mesh=mesh, in_specs=in_specs, out_specs=out_specs, check_vma=False
-    )
+        relay_on_device if fits_relay(mesh) else on_device,
+        mesh=mesh,
+        in_specs=in_specs,
+        out_specs=out_specs,
+        check_vma=False,
+    )

time: 156 us -> 55.1 us (0.35)
  waiting for transfers between devices: 99.3 us -> 0 us
  Pallas kernels: 0 us -> 48.8 us
  matrix products: 24.6 us -> 0 us
  between operations: 14.2 us -> 0.66 us
  other arithmetic: 7.98 us -> 0 us
  starting transfers between devices: 4.29 us -> 0 us
    reduce_scatter x4 -> x0, waiting for transfers between devices: 53.1 us -> none  [the longest x1 38.7 us: on_device(): lax.psum_scatter(term_out.astype(jnp.bfloat16), 'dp', scatter_dimension=1...]
    pallas_call x0 -> x1, Pallas kernels: none -> 48.8 us  [relay_on_device(): pl.pallas_call(relay_kernel, out_shape=(shape((rows, width), bf16), shape...]
    dot_general x6 -> x0, matrix products: 24.6 us -> none  [the longest x1 5.42 us: on_device(): terms = jnp.dot(act, w_second, preferred_element_type=jnp.float32)]
    ppermute x2 -> x0, waiting for transfers between devices: 22.3 us -> none  [shifted(): lax.ppermute(x, axis, [(i, (i + by) % length) for i in range(length)])]
    all_gather x3 -> x0, waiting for transfers between devices: 21.9 us -> none  [the longest x1 11.9 us: on_device(): lax.all_gather(x_bwd, 'mp', axis=0, tiled=True)]
    reduce_sum x3 -> x0, other arithmetic: 4.3 us -> none  [the longest x2 3.01 us: prepare(): scale = lax.rsqrt(jnp.mean(xf * xf, axis=-1, keepdims=True) + norm_eps)]
    ppermute x2 -> x0, starting transfers between devices: 4.01 us -> none  [shifted(): lax.ppermute(x, axis, [(i, (i + by) % length) for i in range(length)])]
    convert_element_type x2 -> x0, other arithmetic: 3.66 us -> none  [the longest x1 2.27 us: on_device(): passed_grad = shifted(dx.astype(jnp.bfloat16), 'section', -1)]
  transfers between devices with their start and end apart: 9 -> 0, of which waited for: 7 -> 0; matrix products, arithmetic and copies ran while one was open for 21% -> 0% of each run, Pallas kernels for 0% -> 0%
where the time goes in v1:
time: 55.1 us; the launch traced here: 54.9 us
  Pallas kernels  48.8 us (89%)
  local copies, waits for them, and re-layouts  5.42 us (10%)
  between operations  0.66 us (1%)
    pallas_call x1, Pallas kernels, relay_on_device(): pl.pallas_call(relay_kernel, out_shape=(shape((rows, width), bf16), shape...  48.8 us
    unnamed x8, local copies, waits for them, and re-layouts  5.42 us

profile of v1, /device:TPU:0, one launch (start us, length us, event | category | flops | bytes accessed | tf_op | source)
XLA Modules:
  0.0 54.9 jit_solution(17506449430887081719)
XLA Ops:
  0.6 48.8 %shard_map.93 = (bf16[256,1024]{1,0:T(8,128)(2,1)}, bf16[256,1024]{1,0:T(8,128)(2,1)}, bf16[1024,256]{1,0:T(8,128)(2,1)}, bf16[1024,256]{1,0:T(8,128)(2,1)}) custom-call(bf16[256,1024]{1,0:T(8,128)(2,1)} %bitcast.11, bf16[256,1024]{1,0:T(8,128)(2,1)} %bitcast.12, bf16[256,1024]{1,0:T(8,128)(2,1)} %bitcast.13, bf16[1024,1024]{1,0:T(8,128)(2,1)} %bitcast.9, ...), custom_call_target="tpu_custom_call" | custom-call | tf_op jit(solution)/shard_map/pallas_call | solution.py:355
  49.4 0.0 copy-start.1
  49.4 0.0 copy-start
  49.5 2.0 %copy.14 = bf16[1,256,1024]{2,1,0:T(8,128)(2,1)} copy(bf16[1,256,1024]{2,1,0:T(8,128)(2,1)} %bitcast.17) | data formatting | bytes 1048576
  51.4 1.9 %copy.15 = bf16[1,256,1024]{2,1,0:T(8,128)(2,1)} copy(bf16[1,256,1024]{2,1,0:T(8,128)(2,1)} %bitcast.16) | data formatting | bytes 1048576
  53.3 0.0 copy-done.1
  53.3 0.8 %copy.16 = bf16[1,1024,256]{2,1,0:T(8,128)(2,1)} copy(bf16[1,1024,256]{2,1,0:T(8,128)(2,1)S(1)} %bitcast.15) | data formatting | bytes 1048576
  54.1 0.0 copy-done
  54.1 0.8 %copy.17 = bf16[1,1024,256]{2,1,0:T(8,128)(2,1)} copy(bf16[1,1024,256]{2,1,0:T(8,128)(2,1)S(1)} %bitcast.14) | data formatting | bytes 1048576
Async XLA Ops:
  49.4 3.8 %copy-start.1 = (bf16[1024,256]{1,0:T(8,128)(2,1)S(1)}, bf16[1024,256]{1,0:T(8,128)(2,1)}, u32[]{:S(2)}) copy-start(bf16[1024,256]{1,0:T(8,128)(2,1)} %get-tuple-element.10) | copy-start | bytes 1572868
  49.4 4.6 %copy-start = (bf16[1024,256]{1,0:T(8,128)(2,1)S(1)}, bf16[1024,256]{1,0:T(8,128)(2,1)}, u32[]{:S(2)}) copy-start(bf16[1024,256]{1,0:T(8,128)(2,1)} %get-tuple-element.11) | copy-start | bytes 1572868

commit v2 on v1

--- a/solution.py
+++ b/solution.py
@@ -103,6 +103,7 @@
 
 
 MESH = pl.DeviceIdType.MESH
+vmem_bytes = 67_043_328
 NT = (((1,), (1,)), ((), ()))
 TN = (((0,), (0,)), ((), ()))
 DIAG, DIRECT, SECOND, OWN = range(4)
@@ -116,15 +117,69 @@
     return size
 
 
-def relay_kernel(
-    fwd_hbm, stash_hbm, cot_hbm, win_hbm, wout_hbm, gain_ref,
-    pass_fwd, pass_grad, gin_ref, gout_ref,
-    xs, xc, xf, nb, nf, win, wout, slope, act_t, dpre_t, act, parts, landed,
-    mp_out, mp_in, own_terms, z_out,
-    load_sem, mp_send, mp_recv, rs_send, rs_recv, z_send, z_recv,
+def start_remote(src, dst, send, recv, target):
+    copy = pltpu.make_async_remote_copy(
+        src_ref=src, dst_ref=dst, send_sem=send, recv_sem=recv,
+        device_id=target, device_id_type=MESH,
+    )
+    copy.start()
+    return copy
+
+
+def greet(targets):
+    barrier = pltpu.get_barrier_semaphore()
+    for target in targets:
+        pl.semaphore_signal(barrier, inc=1, device_id=target, device_id_type=MESH)
+    return barrier
+
+
+def swap_kernel(
+    fwd_hbm, stash_hbm, cot_hbm, win_hbm, wout_hbm,
+    xs, xc, xf, win, wout,
+    load_sem, send_sem, recv_sem,
 ):
     rows = stash_hbm.shape[0]
-    hid, width = win_hbm.shape
+    peer = {"mp": 1 - lax.axis_index("mp")}
+    barrier = greet([peer])
+    own, other = pl.ds(0, rows), pl.ds(rows, rows)
+    shared = ((stash_hbm, xs), (cot_hbm, xc), (fwd_hbm, xf))
+    pairs = [(src, dst.at[own]) for src, dst in shared] + [(win_hbm, win), (wout_hbm, wout)]
+    loads = [
+        pltpu.make_async_copy(src, dst, load_sem.at[i]) for i, (src, dst) in enumerate(pairs)
+    ]
+    pl.semaphore_wait(barrier, 1)
+    swaps = [
+        start_remote(src, dst.at[other], send_sem.at[i], recv_sem.at[i], peer)
+        for i, (src, dst) in enumerate(shared)
+    ]
+    for load in loads:
+        load.start()
+    for load in loads:
+        load.wait()
+    for swap in swaps:
+        swap.wait()
+
+
+def write_kernel(a, b, c, d, a_out, b_out, c_out, d_out, sems):
+    copies = [
+        pltpu.make_async_copy(src, dst, sems.at[i])
+        for i, (src, dst) in enumerate(((a, a_out), (b, b_out), (c, c_out), (d, d_out)))
+    ]
+    for copy in copies:
+        copy.start()
+    for copy in copies:
+        copy.wait()
+
+
+def relay_kernel(
+    xs, xc, xf, win, wout, gain_ref,
+    pass_fwd, pass_grad, gin_ref, gout_ref,
+    nb, nf, slope, act_t, dpre_t, act, parts, landed,
+    mp_out, mp_in, own_terms, z_out,
+    mp_send, mp_recv, rs_send, rs_recv, z_send, z_recv,
+):
+    rows = pass_fwd.shape[0]
+    hid, width = win.shape
     half = hid // 2
     cols = gin_ref.shape[1]
     n_sec = lax.axis_size("section")
@@ -134,36 +189,9 @@
     across = (1 - y) * 2 + (1 - x)
     peer = {"mp": 1 - mp}
     after, before = {"section": lax.rem(sec + 1, n_sec)}, {"section": lax.rem(sec + n_sec - 1, n_sec)}
+    barrier = greet([after, before, {"dp": flip_x}, {"dp": flip_y}, peer])
 
     own, other = pl.ds(0, rows), pl.ds(rows, rows)
-    loads = [
-        pltpu.make_async_copy(stash_hbm, xs.at[own], load_sem.at[0]),
-        pltpu.make_async_copy(win_hbm, win, load_sem.at[1]),
-        pltpu.make_async_copy(cot_hbm, xc.at[own], load_sem.at[2]),
-        pltpu.make_async_copy(wout_hbm, wout, load_sem.at[3]),
-        pltpu.make_async_copy(fwd_hbm, xf.at[own], load_sem.at[4]),
-    ]
-    for load in loads:
-        load.start()
-
-    barrier = pltpu.get_barrier_semaphore()
-    for target in (peer, {"dp": flip_x}, {"dp": flip_y}, after, before):
-        pl.semaphore_signal(barrier, inc=1, device_id=target, device_id_type=MESH)
-    pl.semaphore_wait(barrier, 5)
-
-    def remote(src, dst, send, recv, target):
-        copy = pltpu.make_async_remote_copy(
-            src_ref=src, dst_ref=dst, send_sem=send, recv_sem=recv,
-            device_id=target, device_id_type=MESH,
-        )
-        copy.start()
-        return copy
-
-    swaps = [
-        remote(src, dst.at[other], mp_send.at[i], mp_recv.at[i], peer)
-        for i, (src, dst) in enumerate(((stash_hbm, xs), (cot_hbm, xc), (fwd_hbm, xf)))
-    ]
-
     gain = gain_ref[...]
     step = tile_of(rows, 64)
 
@@ -179,16 +207,16 @@
 
     block = tile_of(half, 256)
 
-    def backward_pre(slot, first, count):
+    def backward_pre(first, count):
         def body(i, carry):
             at = pl.ds(pl.multiple_of(first + i * block, block), block)
             v = lax.dot_general(
-                win[at, :], nb[slot, :], NT, preferred_element_type=jnp.float32
+                win[at, :], nb[...], NT, preferred_element_type=jnp.float32
             )
             square = v * v
             t = jnp.tanh(gelu_coef * (v + 0.044715 * square * v))
-            act_t[at, slot] = (0.5 * v * (1.0 + t)).astype(jnp.bfloat16)
-            slope[at, slot] = 0.5 * (1.0 + t) + 0.5 * v * (1.0 - t * t) * gelu_coef * (
+            act_t[at, :] = (0.5 * v * (1.0 + t)).astype(jnp.bfloat16)
+            slope[at, :] = 0.5 * (1.0 + t) + 0.5 * v * (1.0 - t * t) * gelu_coef * (
                 1.0 + 0.134145 * square
             )
             return carry
@@ -224,31 +252,25 @@
     sent = {}
 
     def send(g, h, kind):
-        sent[g, h, kind] = remote(
+        sent[g, h, kind] = start_remote(
             parts.at[g, h, kind], landed.at[g, h, kind],
             rs_send.at[g, h, kind], rs_recv.at[g, h, kind],
             nearest[h][1 if kind == SECOND else 0],
         )
 
-    loads[0].wait()
     normalise(xs, nb, 0)
-    loads[1].wait()
-    backward_pre(own, 0, hid)
-    swaps[0].wait_recv()
     normalise(xs, nb, rows)
-    backward_pre(other, 0, half)
-    loads[2].wait()
-    swaps[1].wait_recv()
+    backward_pre(0, half)
     product(OUT, 0, DIAG)
+    pl.semaphore_wait(barrier, 5)
     send(OUT, 0, DIAG)
-    backward_pre(other, half, half)
+    backward_pre(half, half)
     product(OUT, 1, DIAG)
     send(OUT, 1, DIAG)
     for h in range(2):
         product(OUT, h, DIRECT)
         send(OUT, h, DIRECT)
 
-    loads[3].wait()
     for h in range(2):
         backward_slope(h * half, half)
         product(IN, h, DIAG)
@@ -263,10 +285,9 @@
         ).astype(jnp.bfloat16)
 
     mp_out[0] = d_norm(other)
-    swap_grad = remote(mp_out.at[0], mp_in.at[0], mp_send.at[3], mp_recv.at[3], peer)
+    swap_grad = start_remote(mp_out.at[0], mp_in.at[0], mp_send.at[0], mp_recv.at[0], peer)
     own_terms[0] = d_norm(own)
 
-    loads[4].wait()
 
     def forward(slot):
         def body(i, carry):
@@ -296,12 +317,11 @@
         return carry
 
     lax.fori_loop(0, rows // step, finish_grad, 0)
-    relay_grad = remote(z_out.at[0], pass_grad, z_send.at[0], z_recv.at[0], before)
-
-    swaps[2].wait_recv()
+    relay_grad = start_remote(z_out.at[0], pass_grad, z_send.at[0], z_recv.at[0], before)
+
     normalise(xf, nf, rows)
     mp_out[1] = forward(other)
-    swap_branch = remote(mp_out.at[1], mp_in.at[1], mp_send.at[4], mp_recv.at[4], peer)
+    swap_branch = start_remote(mp_out.at[1], mp_in.at[1], mp_send.at[1], mp_recv.at[1], peer)
     normalise(xf, nf, 0)
     own_terms[1] = forward(own)
     swap_branch.wait_recv()
@@ -313,7 +333,7 @@
         return carry
 
     lax.fori_loop(0, rows // step, finish_forward, 0)
-    relay_fwd = remote(z_out.at[1], pass_fwd, z_send.at[1], z_recv.at[1], after)
+    relay_fwd = start_remote(z_out.at[1], pass_fwd, z_send.at[1], z_recv.at[1], after)
 
     for g in (OUT, IN):
         for h in range(2):
@@ -338,7 +358,7 @@
 
     relay_grad.wait_recv()
     relay_fwd.wait_recv()
-    for copy in [*swaps, swap_grad, swap_branch, relay_grad, relay_fwd, *sent.values()]:
+    for copy in [swap_grad, swap_branch, relay_grad, relay_fwd, *sent.values()]:
         copy.wait_send()
 
 
@@ -351,23 +371,28 @@
     bf16 = jnp.bfloat16
     vmem = pl.BlockSpec(memory_space=pltpu.VMEM)
     hbm = pl.BlockSpec(memory_space=pl.ANY)
-    shape = jax.ShapeDtypeStruct
+    dma = pltpu.SemaphoreType.DMA
+    held = (tokens * 3 + hid * 2) * width * jnp.dtype(bf16).itemsize
+    loaded = pl.pallas_call(
+        swap_kernel,
+        out_shape=(pltpu.VMEM((tokens, width), bf16),) * 3
+        + (pltpu.VMEM((hid, width), bf16),) * 2,
+        in_specs=[hbm] * 5,
+        out_specs=(vmem,) * 5,
+        scratch_shapes=[dma((5,)), dma((3,)), dma((3,))],
+        compiler_params=pltpu.CompilerParams(
+            collective_id=0, has_side_effects=True,
+            vmem_limit_bytes=vmem_bytes - held - 2**17,
+        ),
+    )(fwd_in[0], stash[0], cot[0], w_in[0], w_out[0])
     results = pl.pallas_call(
         relay_kernel,
-        out_shape=(
-            shape((rows, width), bf16), shape((rows, width), bf16),
-            shape((hid, cols), bf16), shape((hid, cols), bf16),
-        ),
-        in_specs=[hbm] * 5 + [vmem],
+        out_shape=(pltpu.VMEM((rows, width), bf16),) * 2 + (pltpu.VMEM((hid, cols), bf16),) * 2,
+        in_specs=[vmem] * 6,
         out_specs=(vmem,) * 4,
         scratch_shapes=[
             pltpu.VMEM((tokens, width), bf16),
             pltpu.VMEM((tokens, width), bf16),
-            pltpu.VMEM((tokens, width), bf16),
-            pltpu.VMEM((tokens, width), bf16),
-            pltpu.VMEM((tokens, width), bf16),
-            pltpu.VMEM((hid, width), bf16),
-            pltpu.VMEM((hid, width), bf16),
             pltpu.VMEM((hid, tokens), jnp.float32),
             pltpu.VMEM((hid, tokens), bf16),
             pltpu.VMEM((hid, tokens), bf16),
@@ -378,18 +403,25 @@
             pltpu.VMEM((2, rows, width), bf16),
             pltpu.VMEM((2, rows, width), bf16),
             pltpu.VMEM((2, rows, width), bf16),
-            pltpu.SemaphoreType.DMA((5,)),
-            pltpu.SemaphoreType.DMA((5,)),
-            pltpu.SemaphoreType.DMA((5,)),
-            pltpu.SemaphoreType.DMA((2, 2, 3)),
-            pltpu.SemaphoreType.DMA((2, 2, 3)),
-            pltpu.SemaphoreType.DMA((2,)),
-            pltpu.SemaphoreType.DMA((2,)),
+            dma((2,)),
+            dma((2,)),
+            dma((2, 2, 3)),
+            dma((2, 2, 3)),
+            dma((2,)),
+            dma((2,)),
         ],
         compiler_params=pltpu.CompilerParams(
-            collective_id=0, has_side_effects=True, vmem_limit_bytes=56 * 2**20
+            collective_id=1, has_side_effects=True, vmem_limit_bytes=40 * 2**20
         ),
-    )(fwd_in[0], stash[0], cot[0], w_in[0], w_out[0], gain)
+    )(*loaded, gain)
+    results = pl.pallas_call(
+        write_kernel,
+        out_shape=tuple(jax.ShapeDtypeStruct(r.shape, r.dtype) for r in results),
+        in_specs=[vmem] * 4,
+        out_specs=(hbm,) * 4,
+        scratch_shapes=[dma((4,))],
+        compiler_params=pltpu.CompilerParams(vmem_limit_bytes=4 * 2**20),
+    )(*results)
     return tuple(r[None] for r in results)
 
 

time: 55.1 us -> 49.2 us (0.89)
  local copies, waits for them, and re-layouts: 5.42 us -> 0.01 us
    unnamed x8 -> x2, local copies, waits for them, and re-layouts: 5.42 us -> 0.01 us
    pallas_call x1 -> x3, Pallas kernels: 48.8 us -> 48.4 us  [the longest x1 43.2 us: relay_on_device(): pl.pallas_call(relay_kernel, out_shape=(pltpu.VMEM((rows, width), bf16),)...]
where the time goes in v2:
time: 49.2 us; the launch traced here: 49 us
  Pallas kernels  48.4 us (98%)
  between operations  0.66 us (1%)
    pallas_call x1, Pallas kernels, relay_on_device(): pl.pallas_call(relay_kernel, out_shape=(pltpu.VMEM((rows, width), bf16),)...  43.2 us
    pallas_call x1, Pallas kernels, relay_on_device(): pl.pallas_call(swap_kernel, out_shape=(pltpu.VMEM((tokens, width), bf16),...  3.86 us
    pallas_call x1, Pallas kernels, relay_on_device(): pl.pallas_call(write_kernel, out_shape=tuple((jax.ShapeDtypeStruct(r.shap...  1.35 us

profile of v2, /device:TPU:0, one launch (start us, length us, event | category | flops | bytes accessed | tf_op | source)
XLA Modules:
  0.0 49.0 jit_solution(10693164181503724115)
XLA Ops:
  0.6 0.0 copy-start
  0.6 3.9 %shard_map.93 = (bf16[512,1024]{1,0:T(8,128)(2,1)S(1)}, bf16[512,1024]{1,0:T(8,128)(2,1)S(1)}, bf16[512,1024]{1,0:T(8,128)(2,1)S(1)}, bf16[1024,1024]{1,0:T(8,128)(2,1)S(1)}, bf16[1024,1024]{1,0:T(8,128)(2,1)S(1)}) custom-call(bf16[256,1024]{1,0:T(8,128)(2,1)} %bitcast.11, bf16[256,1024]{1,0:T(8,128)(2,1)} %bitcast.12, bf16[256,1024]{1,0:T(8,128)(2,1)} %bitcast.13, ...), custom_call_target="tpu_custom_call" | custom-call | tf_op jit(solution)/shard_map/pallas_call | solution.py:376
  4.5 0.0 copy-done
  4.5 43.2 %shard_map.94 = (bf16[256,1024]{1,0:T(8,128)(2,1)S(1)}, bf16[256,1024]{1,0:T(8,128)(2,1)S(1)}, bf16[1024,256]{1,0:T(8,128)(2,1)S(1)}, bf16[1024,256]{1,0:T(8,128)(2,1)S(1)}) custom-call(bf16[512,1024]{1,0:T(8,128)(2,1)S(1)} %get-tuple-element.17.xs, bf16[512,1024]{1,0:T(8,128)(2,1)S(1)} %get-tuple-element.18.xc, bf16[512,1024]{1,0:T(8,128)(2,1)S(1)} %get-tuple-element.19.xf, ...), custom_call_target="tpu_custom_call" | custom-call | tf_op jit(solution)/shard_map/pallas_call | solution.py:388
  47.7 1.3 %shard_map.95 = (bf16[256,1024]{1,0:T(8,128)(2,1)}, bf16[256,1024]{1,0:T(8,128)(2,1)}, bf16[1024,256]{1,0:T(8,128)(2,1)}, bf16[1024,256]{1,0:T(8,128)(2,1)}) custom-call(bf16[256,1024]{1,0:T(8,128)(2,1)S(1)} %get-tuple-element.22.a, bf16[256,1024]{1,0:T(8,128)(2,1)S(1)} %get-tuple-element.23.b, bf16[1024,256]{1,0:T(8,128)(2,1)S(1)} %get-tuple-element.24.c, ...), custom_call_target="tpu_custom_call" | custom-call | tf_op jit(solution)/shard_map/pallas_call | solution.py:417
Async XLA Ops:
  0.6 3.9 %copy-start = (f32[1,1024]{1,0:T(1,128)S(1)}, f32[1,1024]{1,0:T(1,128)}, u32[]{:S(2)}) copy-start(f32[1,1024]{1,0:T(1,128)} %gain_ref.1) | copy-start | bytes 12292

commit v3 on v2

--- a/solution.py
+++ b/solution.py
@@ -142,8 +142,9 @@
     peer = {"mp": 1 - lax.axis_index("mp")}
     barrier = greet([peer])
     own, other = pl.ds(0, rows), pl.ds(rows, rows)
-    shared = ((stash_hbm, xs), (cot_hbm, xc), (fwd_hbm, xf))
-    pairs = [(src, dst.at[own]) for src, dst in shared] + [(win_hbm, win), (wout_hbm, wout)]
+    shared = ((stash_hbm, xs), (cot_hbm, xc))
+    whole = ((win_hbm, win), (fwd_hbm, xf), (wout_hbm, wout))
+    pairs = [*((src, dst.at[own]) for src, dst in shared), *whole]
     loads = [
         pltpu.make_async_copy(src, dst, load_sem.at[i]) for i, (src, dst) in enumerate(pairs)
     ]
@@ -174,7 +175,7 @@
 def relay_kernel(
     xs, xc, xf, win, wout, gain_ref,
     pass_fwd, pass_grad, gin_ref, gout_ref,
-    nb, nf, slope, act_t, dpre_t, act, parts, landed,
+    xf_peer, nb, nf, slope, act_t, dpre_t, act, parts, landed,
     mp_out, mp_in, own_terms, z_out,
     mp_send, mp_recv, rs_send, rs_recv, z_send, z_recv,
 ):
@@ -195,10 +196,10 @@
     gain = gain_ref[...]
     step = tile_of(rows, 64)
 
-    def normalise(source, target, first):
+    def normalise(source, target, first, skip=0):
         def body(i, carry):
             at = pl.ds(pl.multiple_of(first + i * step, step), step)
-            v = source[at, :].astype(jnp.float32)
+            v = source[pl.ds(pl.multiple_of(first - skip + i * step, step), step), :].astype(jnp.float32)
             r = lax.rsqrt(jnp.mean(v * v, axis=-1, keepdims=True) + norm_eps)
             target[at, :] = (v * r * gain).astype(jnp.bfloat16)
             return carry
@@ -262,11 +263,12 @@
     normalise(xs, nb, rows)
     backward_pre(0, half)
     product(OUT, 0, DIAG)
+    backward_pre(half, half)
+    product(OUT, 1, DIAG)
     pl.semaphore_wait(barrier, 5)
     send(OUT, 0, DIAG)
-    backward_pre(half, half)
-    product(OUT, 1, DIAG)
     send(OUT, 1, DIAG)
+    swap_fwd = start_remote(xf, xf_peer, mp_send.at[2], mp_recv.at[2], peer)
     for h in range(2):
         product(OUT, h, DIRECT)
         send(OUT, h, DIRECT)
@@ -319,7 +321,8 @@
     lax.fori_loop(0, rows // step, finish_grad, 0)
     relay_grad = start_remote(z_out.at[0], pass_grad, z_send.at[0], z_recv.at[0], before)
 
-    normalise(xf, nf, rows)
+    swap_fwd.wait_recv()
+    normalise(xf_peer, nf, rows, rows)
     mp_out[1] = forward(other)
     swap_branch = start_remote(mp_out.at[1], mp_in.at[1], mp_send.at[1], mp_recv.at[1], peer)
     normalise(xf, nf, 0)
@@ -358,7 +361,7 @@
 
     relay_grad.wait_recv()
     relay_fwd.wait_recv()
-    for copy in [swap_grad, swap_branch, relay_grad, relay_fwd, *sent.values()]:
+    for copy in [swap_fwd, swap_grad, swap_branch, relay_grad, relay_fwd, *sent.values()]:
         copy.wait_send()
 
 
@@ -372,14 +375,15 @@
     vmem = pl.BlockSpec(memory_space=pltpu.VMEM)
     hbm = pl.BlockSpec(memory_space=pl.ANY)
     dma = pltpu.SemaphoreType.DMA
-    held = (tokens * 3 + hid * 2) * width * jnp.dtype(bf16).itemsize
+    held = (tokens * 2 + rows + hid * 2) * width * jnp.dtype(bf16).itemsize
     loaded = pl.pallas_call(
         swap_kernel,
-        out_shape=(pltpu.VMEM((tokens, width), bf16),) * 3
+        out_shape=(pltpu.VMEM((tokens, width), bf16),) * 2
+        + (pltpu.VMEM((rows, width), bf16),)
         + (pltpu.VMEM((hid, width), bf16),) * 2,
         in_specs=[hbm] * 5,
         out_specs=(vmem,) * 5,
-        scratch_shapes=[dma((5,)), dma((3,)), dma((3,))],
+        scratch_shapes=[dma((5,)), dma((2,)), dma((2,))],
         compiler_params=pltpu.CompilerParams(
             collective_id=0, has_side_effects=True,
             vmem_limit_bytes=vmem_bytes - held - 2**17,
@@ -391,6 +395,7 @@
         in_specs=[vmem] * 6,
         out_specs=(vmem,) * 4,
         scratch_shapes=[
+            pltpu.VMEM((rows, width), bf16),
             pltpu.VMEM((tokens, width), bf16),
             pltpu.VMEM((tokens, width), bf16),
             pltpu.VMEM((hid, tokens), jnp.float32),
@@ -403,8 +408,8 @@
             pltpu.VMEM((2, rows, width), bf16),
             pltpu.VMEM((2, rows, width), bf16),
             pltpu.VMEM((2, rows, width), bf16),
-            dma((2,)),
-            dma((2,)),
+            dma((3,)),
+            dma((3,)),
             dma((2, 2, 3)),
             dma((2, 2, 3)),
             dma((2,)),

time: 49.2 us -> 48.1 us (0.978)
  Pallas kernels: 48.4 us -> 47.3 us
    pallas_call x1, Pallas kernels: 3.86 us -> 3.31 us  [relay_on_device(): pl.pallas_call(swap_kernel, out_shape=(pltpu.VMEM((tokens, width), bf16),...]
    pallas_call x1, Pallas kernels: 43.2 us -> 42.6 us  [relay_on_device(): pl.pallas_call(relay_kernel, out_shape=(pltpu.VMEM((rows, width), bf16),)...]
where the time goes in v3:
time: 48.1 us; the launch traced here: 48 us
  Pallas kernels  47.3 us (98%)
  between operations  0.66 us (1%)
    pallas_call x1, Pallas kernels, relay_on_device(): pl.pallas_call(relay_kernel, out_shape=(pltpu.VMEM((rows, width), bf16),)...  42.6 us
    pallas_call x1, Pallas kernels, relay_on_device(): pl.pallas_call(swap_kernel, out_shape=(pltpu.VMEM((tokens, width), bf16),...  3.31 us
    pallas_call x1, Pallas kernels, relay_on_device(): pl.pallas_call(write_kernel, out_shape=tuple((jax.ShapeDtypeStruct(r.shap...  1.35 us

profile of v3, /device:TPU:0, one launch (start us, length us, event | category | flops | bytes accessed | tf_op | source)
XLA Modules:
  0.0 48.0 jit_solution(14129396857896834422)
XLA Ops:
  0.6 0.0 copy-start
  0.6 3.3 %shard_map.93 = (bf16[512,1024]{1,0:T(8,128)(2,1)S(1)}, bf16[512,1024]{1,0:T(8,128)(2,1)S(1)}, bf16[256,1024]{1,0:T(8,128)(2,1)S(1)}, bf16[1024,1024]{1,0:T(8,128)(2,1)S(1)}, bf16[1024,1024]{1,0:T(8,128)(2,1)S(1)}) custom-call(bf16[256,1024]{1,0:T(8,128)(2,1)} %bitcast.11, bf16[256,1024]{1,0:T(8,128)(2,1)} %bitcast.12, bf16[256,1024]{1,0:T(8,128)(2,1)} %bitcast.13, ...), custom_call_target="tpu_custom_call" | custom-call | tf_op jit(solution)/shard_map/pallas_call | solution.py:379
  4.0 0.0 copy-done
  4.0 42.6 %shard_map.94 = (bf16[256,1024]{1,0:T(8,128)(2,1)S(1)}, bf16[256,1024]{1,0:T(8,128)(2,1)S(1)}, bf16[1024,256]{1,0:T(8,128)(2,1)S(1)}, bf16[1024,256]{1,0:T(8,128)(2,1)S(1)}) custom-call(bf16[512,1024]{1,0:T(8,128)(2,1)S(1)} %get-tuple-element.17.xs, bf16[512,1024]{1,0:T(8,128)(2,1)S(1)} %get-tuple-element.18.xc, bf16[256,1024]{1,0:T(8,128)(2,1)S(1)} %get-tuple-element.19.xf, ...), custom_call_target="tpu_custom_call" | custom-call | tf_op jit(solution)/shard_map/pallas_call | solution.py:392
  46.6 1.3 %shard_map.95 = (bf16[256,1024]{1,0:T(8,128)(2,1)}, bf16[256,1024]{1,0:T(8,128)(2,1)}, bf16[1024,256]{1,0:T(8,128)(2,1)}, bf16[1024,256]{1,0:T(8,128)(2,1)}) custom-call(bf16[256,1024]{1,0:T(8,128)(2,1)S(1)} %get-tuple-element.22.a, bf16[256,1024]{1,0:T(8,128)(2,1)S(1)} %get-tuple-element.23.b, bf16[1024,256]{1,0:T(8,128)(2,1)S(1)} %get-tuple-element.24.c, ...), custom_call_target="tpu_custom_call" | custom-call | tf_op jit(solution)/shard_map/pallas_call | solution.py:422
Async XLA Ops:
  0.6 3.3 %copy-start = (f32[1,1024]{1,0:T(1,128)S(1)}, f32[1,1024]{1,0:T(1,128)}, u32[]{:S(2)}) copy-start(f32[1,1024]{1,0:T(1,128)} %gain_ref.1) | copy-start | bytes 12292
